TPU v7x, 32 devices: a whole 2x2x4 slice. The times are simulated.
32 devices in a mesh: dp: 8 (over y, x, core), tensor: 4 (over z).
Axes of the slice: x: 2, y: 2, z: 4, core: 2. Of those that a mesh axis runs over, the one named last changes fastest.
Arguments:
- tokens_in: bfloat16 [8192, 1536], P('dp'), may hold values from -6 to 6
- doc_ids: int32 [8192], replicated, may hold values from 0 to 3, never falling along the last dimension, each value on 1 to 4096 neighbouring positions
- out_grad: bfloat16 [8192, 1536], P('dp'), may hold values from -6 to 6
- norm_gains: bfloat16 [2, 1536], replicated, may hold values from 0.5 to 1.5
- conv_taps: bfloat16 [3, 1536], P(None, 'tensor'), may hold values from -3.5 to 3.5
- stream_weight: bfloat16 [3, 1536, 1536], P(None, None, 'tensor'), may hold values from -0.15625 to 0.15625
- mixer_weight: bfloat16 [1536, 1536], P('tensor'), may hold values from -0.15625 to 0.15625
- hidden_weight: bfloat16 [2, 1536, 6912], P(None, None, 'tensor'), may hold values from -0.15625 to 0.15625
- down_weight: bfloat16 [6912, 1536], P('tensor'), may hold values from -0.078125 to 0.078125
- gains_first: float32 [2, 1536], replicated, may hold values from -0.0009336855 to 0.0009336855
- gains_second: float32 [2, 1536], replicated, may hold values from 7.2647386e-09 to 7.264739e-08
- taps_first: float32 [3, 1536], P(None, 'tensor'), may hold values from -0.0009336855 to 0.0009336855
- taps_second: float32 [3, 1536], P(None, 'tensor'), may hold values from 7.2647386e-09 to 7.264739e-08
- stream_first: float32 [3, 1536, 1536], P(None, 'dp', 'tensor'), may hold values from -0.0009336855 to 0.0009336855
- stream_second: float32 [3, 1536, 1536], P(None, 'dp', 'tensor'), may hold values from 7.2647386e-09 to 7.264739e-08
- mixer_first: float32 [1536, 1536], P('tensor', 'dp'), may hold values from -0.0009336855 to 0.0009336855
- mixer_second: float32 [1536, 1536], P('tensor', 'dp'), may hold values from 7.2647386e-09 to 7.264739e-08
- hidden_first: float32 [2, 1536, 6912], P(None, 'dp', 'tensor'), may hold values from -0.0009336855 to 0.0009336855
- hidden_second: float32 [2, 1536, 6912], P(None, 'dp', 'tensor'), may hold values from 7.2647386e-09 to 7.264739e-08
- down_first: float32 [6912, 1536], P('tensor', 'dp'), may hold values from -0.0009336855 to 0.0009336855
- down_second: float32 [6912, 1536], P('tensor', 'dp'), may hold values from 7.2647386e-09 to 7.264739e-08
Outputs:
- block_out: bfloat16 [8192, 1536], P('dp')
- input_grad: float32 [8192, 1536], P('dp')
- grad_norm: float32 [], replicated
- gains_grad: float32 [2, 1536], replicated
- gains_first_next: float32 [2, 1536], replicated
- gains_second_next: float32 [2, 1536], replicated
- gains_step: float32 [2, 1536], replicated
- taps_grad: float32 [3, 1536], P(None, 'tensor')
- taps_first_next: float32 [3, 1536], P(None, 'tensor')
- taps_second_next: float32 [3, 1536], P(None, 'tensor')
- taps_step: float32 [3, 1536], P(None, 'tensor')
- stream_grad: float32 [3, 1536, 1536], P(None, 'dp', 'tensor')
- stream_first_next: float32 [3, 1536, 1536], P(None, 'dp', 'tensor')
- stream_second_next: float32 [3, 1536, 1536], P(None, 'dp', 'tensor')
- stream_step: float32 [3, 1536, 1536], P(None, 'dp', 'tensor')
- mixer_grad: float32 [1536, 1536], P('tensor', 'dp')
- mixer_first_next: float32 [1536, 1536], P('tensor', 'dp')
- mixer_second_next: float32 [1536, 1536], P('tensor', 'dp')
- mixer_step: float32 [1536, 1536], P('tensor', 'dp')
- hidden_grad: float32 [2, 1536, 6912], P(None, 'dp', 'tensor')
- hidden_first_next: float32 [2, 1536, 6912], P(None, 'dp', 'tensor')
- hidden_second_next: float32 [2, 1536, 6912], P(None, 'dp', 'tensor')
- hidden_step: float32 [2, 1536, 6912], P(None, 'dp', 'tensor')
- down_grad: float32 [6912, 1536], P('tensor', 'dp')
- down_first_next: float32 [6912, 1536], P('tensor', 'dp')
- down_second_next: float32 [6912, 1536], P('tensor', 'dp')
- down_step: float32 [6912, 1536], P('tensor', 'dp')
Inputs may be any that keep to these rules, and one draw needn't show every extreme that they name: `doc_ids`: document ids never fall along the tokens; each document has 1 to 4096 tokens, and one has exactly 4096.
All inputs are finite; a program needn't handle non-finite values.
Results may differ from a plain program's by a relative error of at most 0.01.
The roundings to bfloat16 on the way count: a program that leaves them out, or rounds other values in their place, can miss the bound.
Values may be sent and summed in bfloat16 or wider, within the bound.
A program may use at most 256 MiB of HBM per device.

v0:
```python
import jax
import jax.numpy as jnp
from jax import lax
from jax.sharding import PartitionSpec as P

EPS_NORM = 1e-05
LEARN_RATE = 0.02
BETA_FIRST = 0.5
BETA_SECOND = 0.5
CORRECTION = 1.0 - 0.5**3
ADAM_EPS = 1e-08
DECAY_RATE = 0.1
CLIP_NORM = 1.0


def shifted(value, axis, steps):
    count = lax.axis_size(axis)
    leading, last = (max(0, -steps), min(count, count - steps))
    return lax.ppermute(value, axis, [(source, source + steps) for source in range(leading, last)])


def rms_scale(values):
    return lax.rsqrt(jnp.mean(values * values, axis=-1, keepdims=True) + EPS_NORM)


def norm_back(grad_normed, normal, inverse, gain_row):
    scaled = grad_normed * gain_row
    return inverse * (scaled - normal * jnp.mean(scaled * normal, axis=-1, keepdims=True))


def adam_step(master, gradient, first_moment, second_moment, factor, decay):
    clipped = gradient * factor
    first_next = BETA_FIRST * first_moment + (1.0 - BETA_FIRST) * clipped
    second_next = BETA_SECOND * second_moment + (1.0 - BETA_SECOND) * clipped * clipped
    change = -LEARN_RATE * (
        first_next / CORRECTION / (jnp.sqrt(second_next / CORRECTION) + ADAM_EPS) + decay * master
    )
    return (first_next, second_next, change)


def own_share(weight, share):
    offset_row = lax.axis_index("dp") * share
    return lax.dynamic_slice_in_dim(weight, offset_row, share, 1).astype(jnp.float32)


def contract_rows(left, right):
    return lax.dot_general(
        left, right, (((0,), (0,)), ((), ())), preferred_element_type=jnp.float32
    )


def contract_cols(left, right):
    return lax.dot_general(
        left, right, (((1,), (1,)), ((), ())), preferred_element_type=jnp.float32
    )


def squares(values):
    return jnp.sum(values * values)


def body(
    tokens_in,
    doc_ids,
    out_grad,
    norm_gains,
    conv_taps,
    stream_weight,
    mixer_weight,
    hidden_weight,
    down_weight,
    gains_first,
    gains_second,
    taps_first,
    taps_second,
    stream_first,
    stream_second,
    mixer_first,
    mixer_second,
    hidden_first,
    hidden_second,
    down_first,
    down_second,
):
    tok_rows = tokens_in.shape[0]
    kernel = conv_taps.shape[0]
    reach = kernel - 1
    first_row = lax.axis_index("dp") * tok_rows
    filler = jnp.full((reach,), -1, jnp.int32)
    padded_ids = jnp.concatenate([filler, doc_ids, filler])
    window = lax.dynamic_slice_in_dim(padded_ids, first_row, tok_rows + 2 * reach)
    current = window[reach : reach + tok_rows]
    back_valid = [
        (window[reach - offset : reach - offset + tok_rows] == current).astype(jnp.float32)[:, None]
        for offset in range(kernel)
    ]
    ahead_valid = [
        (window[reach + offset : reach + offset + tok_rows] == current).astype(jnp.float32)[:, None]
        for offset in range(kernel)
    ]
    tokens = tokens_in.astype(jnp.float32)
    gain_pair = norm_gains.astype(jnp.float32)
    tap_values = conv_taps.astype(jnp.float32)
    scale_one = rms_scale(tokens)
    normal_one = tokens * scale_one
    normed_one = (normal_one * gain_pair[0]).astype(jnp.bfloat16)
    streams = jnp.einsum(
        "td,sdc->stc", normed_one, stream_weight, preferred_element_type=jnp.float32
    )
    product = (streams[0] * streams[2]).astype(jnp.bfloat16)
    edge_rows = shifted(product[tok_rows - reach :], "dp", 1)
    extended = jnp.concatenate([edge_rows, product], 0).astype(jnp.float32)
    conv_out = tap_values[0] * extended[reach : reach + tok_rows] * back_valid[0]
    for offset in range(1, kernel):
        conv_out = (
            conv_out
            + tap_values[offset]
            * extended[reach - offset : reach - offset + tok_rows]
            * back_valid[offset]
        )
    gated_rows = (streams[1] * conv_out).astype(jnp.bfloat16)
    branch_part = jnp.dot(gated_rows, mixer_weight, preferred_element_type=jnp.float32)
    branch = lax.psum(branch_part, "tensor")
    middle = tokens + branch
    scale_two = rms_scale(middle)
    normal_two = middle * scale_two
    normed_two = (normal_two * gain_pair[1]).astype(jnp.bfloat16)
    hidden = jnp.einsum(
        "td,sdf->stf", normed_two, hidden_weight, preferred_element_type=jnp.float32
    )
    sigmoid_gate = jax.nn.sigmoid(hidden[0])
    silu_gate = hidden[0] * sigmoid_gate
    active = (silu_gate * hidden[1]).astype(jnp.bfloat16)
    feed_part = jnp.dot(active, down_weight, preferred_element_type=jnp.float32)
    feed_out = lax.psum(feed_part.astype(jnp.bfloat16), "tensor").astype(jnp.float32)
    block_out = (middle + feed_out).astype(jnp.bfloat16)
    upstream = out_grad.astype(jnp.float32)
    down_part = contract_rows(active, out_grad)
    grad_active = contract_cols(out_grad, down_weight)
    grad_gate = grad_active * hidden[1] * sigmoid_gate * (1.0 + hidden[0] * (1.0 - sigmoid_gate))
    grad_up = grad_active * silu_gate
    grad_hidden = jnp.stack([grad_gate, grad_up]).astype(jnp.bfloat16)
    hidden_part = jnp.einsum(
        "td,stf->sdf", normed_two, grad_hidden, preferred_element_type=jnp.float32
    )
    normed_two_part = jnp.einsum(
        "stf,sdf->td", grad_hidden, hidden_weight, preferred_element_type=jnp.float32
    )
    grad_normed_two = lax.psum(normed_two_part, "tensor")
    gain_two_part = jnp.sum(grad_normed_two * normal_two, axis=0)
    grad_middle = upstream + norm_back(grad_normed_two, normal_two, scale_two, gain_pair[1])
    grad_branch = grad_middle.astype(jnp.bfloat16)
    mixer_part = contract_rows(gated_rows, grad_branch)
    grad_gated = contract_cols(grad_branch, mixer_weight)
    grad_c = grad_gated * conv_out
    grad_conv = (grad_gated * streams[1]).astype(jnp.bfloat16)
    ahead_rows = shifted(grad_conv[:reach], "dp", -1)
    trailing = jnp.concatenate([grad_conv, ahead_rows], 0).astype(jnp.float32)
    grad_conv_wide = trailing[:tok_rows]
    taps_part = jnp.stack(
        [
            jnp.sum(
                grad_conv_wide
                * extended[reach - offset : reach - offset + tok_rows]
                * back_valid[offset],
                axis=0,
            )
            for offset in range(kernel)
        ]
    )
    grad_product = tap_values[0] * grad_conv_wide * ahead_valid[0]
    for offset in range(1, kernel):
        grad_product = (
            grad_product
            + tap_values[offset] * trailing[offset : offset + tok_rows] * ahead_valid[offset]
        )
    grad_streams = jnp.stack([grad_product * streams[2], grad_c, grad_product * streams[0]]).astype(
        jnp.bfloat16
    )
    stream_part = jnp.einsum(
        "td,stc->sdc", normed_one, grad_streams, preferred_element_type=jnp.float32
    )
    normed_one_part = jnp.einsum(
        "stc,sdc->td", grad_streams, stream_weight, preferred_element_type=jnp.float32
    )
    grad_normed_one = lax.psum(normed_one_part, "tensor")
    gain_one_part = jnp.sum(grad_normed_one * normal_one, axis=0)
    input_grad = grad_middle + norm_back(grad_normed_one, normal_one, scale_one, gain_pair[0])
    gain_stack = jnp.stack([gain_one_part, gain_two_part])
    gains_grad, taps_grad = lax.psum((gain_stack, taps_part), "dp")
    stream_total, mixer_total, hidden_total, down_total = (
        lax.psum_scatter(stream_part, "dp", scatter_dimension=1, tiled=True),
        lax.psum_scatter(mixer_part, "dp", scatter_dimension=1, tiled=True),
        lax.psum_scatter(hidden_part, "dp", scatter_dimension=1, tiled=True),
        lax.psum_scatter(down_part, "dp", scatter_dimension=1, tiled=True),
    )
    first_dp = (lax.axis_index("dp") == 0).astype(jnp.float32)
    first_tensor = (lax.axis_index("tensor") == 0).astype(jnp.float32)
    local_square = (
        squares(stream_total) + squares(mixer_total) + squares(hidden_total) + squares(down_total)
    )
    local_square = local_square + first_dp * (
        squares(taps_grad) + first_tensor * squares(gains_grad)
    )
    square_total = lax.psum(local_square, ("dp", "tensor"))
    grad_norm = jnp.sqrt(square_total)
    factor = jnp.minimum(1.0, CLIP_NORM / (grad_norm + 1e-06))
    gains_out = adam_step(gain_pair, gains_grad, gains_first, gains_second, factor, 0.0)
    taps_out = adam_step(tap_values, taps_grad, taps_first, taps_second, factor, DECAY_RATE)
    stream_out = adam_step(
        own_share(stream_weight, stream_total.shape[1]),
        stream_total,
        stream_first,
        stream_second,
        factor,
        DECAY_RATE,
    )
    mixer_out = adam_step(
        own_share(mixer_weight, mixer_total.shape[1]),
        mixer_total,
        mixer_first,
        mixer_second,
        factor,
        DECAY_RATE,
    )
    hidden_out = adam_step(
        own_share(hidden_weight, hidden_total.shape[1]),
        hidden_total,
        hidden_first,
        hidden_second,
        factor,
        DECAY_RATE,
    )
    down_out = adam_step(
        own_share(down_weight, down_total.shape[1]),
        down_total,
        down_first,
        down_second,
        factor,
        DECAY_RATE,
    )
    return (
        block_out,
        input_grad,
        grad_norm,
        gains_grad,
        gains_out[0],
        gains_out[1],
        gains_out[2],
        taps_grad,
        taps_out[0],
        taps_out[1],
        taps_out[2],
        stream_total,
        stream_out[0],
        stream_out[1],
        stream_out[2],
        mixer_total,
        mixer_out[0],
        mixer_out[1],
        mixer_out[2],
        hidden_total,
        hidden_out[0],
        hidden_out[1],
        hidden_out[2],
        down_total,
        down_out[0],
        down_out[1],
        down_out[2],
    )


def solution(mesh):
    return jax.shard_map(
        body,
        mesh=mesh,
        in_specs=(
            P("dp", None),
            P(),
            P("dp", None),
            P(),
            P(None, "tensor"),
            P(None, None, "tensor"),
            P("tensor", None),
            P(None, None, "tensor"),
            P("tensor", None),
            P(),
            P(),
            P(None, "tensor"),
            P(None, "tensor"),
            P(None, "dp", "tensor"),
            P(None, "dp", "tensor"),
            P("tensor", "dp"),
            P("tensor", "dp"),
            P(None, "dp", "tensor"),
            P(None, "dp", "tensor"),
            P("tensor", "dp"),
            P("tensor", "dp"),
        ),
        out_specs=(
            P("dp", None),
            P("dp", None),
            P(),
            P(),
            P(),
            P(),
            P(),
            P(None, "tensor"),
            P(None, "tensor"),
            P(None, "tensor"),
            P(None, "tensor"),
            P(None, "dp", "tensor"),
            P(None, "dp", "tensor"),
            P(None, "dp", "tensor"),
            P(None, "dp", "tensor"),
            P("tensor", "dp"),
            P("tensor", "dp"),
            P("tensor", "dp"),
            P("tensor", "dp"),
            P(None, "dp", "tensor"),
            P(None, "dp", "tensor"),
            P(None, "dp", "tensor"),
            P(None, "dp", "tensor"),
            P("tensor", "dp"),
            P("tensor", "dp"),
            P("tensor", "dp"),
            P("tensor", "dp"),
        ),
        check_vma=False,
    )
```

profile of v0, /device:TPU:0, one launch (start us, length us, event | category | flops | bytes accessed | tf_op | source)
XLA Modules:
  0.0 1472.9 jit_solution(3615150835446457697)
XLA Ops:
  11.3 4.3 convolution_bitcast_fusion.4
  32.0 4.5 fusion.54
  36.8 224.8 %all-reduce.8.cloned.1.call-done = f32[1024,1536]{1,0:T(8,128)} async-done(((f32[1024,1536]{1,0:T(8,128)}), f32[1024,1536]{1,0:T(8,128)}) %all-reduce.8.cloned.1.call-update) | async-done | bytes 6291472 | tf_op jit(solution)/shard_map/psum | solution.py:123
  261.6 4.6 multiply_reduce_fusion.2
  268.9 17.3 %convolution_bitcast_fusion.1 = f32[2,1024,1728]{1,2,0:T(8,128)} fusion(bf16[2,1536,1728]{1,2,0:T(8,128)(2,1)} %param.28, f32[1024,1536]{1,0:T(8,128)S(1)} %get-tuple-element.146, f32[1536]{0:T(1024)S(1)} %get-tuple-element.115, f32[1024]{0:T(1024)S(1)} %add_rsqrt_fusion), kind=kOutput, calls=%fused_computation.16 | convolution fusion | flops 10876354560 | bytes 31074304 | tf_op jit(solution)/shard_map/td,sdf->stf/dot_general | solution.py:128
  286.2 16.0 %fusion.15 = (bf16[1,1024,1728]{1,2,0:T(8,128)(2,1)}, bf16[1,1024,1728]{1,2,0:T(8,128)(2,1)}, bf16[1024,1728]{0,1:T(8,128)(2,1)}) fusion(f32[2,1024,1728]{1,2,0:T(8,128)} %convolution_bitcast_fusion.1, bf16[1024,1536]{1,0:T(8,128)(2,1)S(1)} %copy-done.13, bf16[1728,1536]{1,0:T(8,128)(2,1)} %param.29), kind=kOutput, calls=%fused_computation.38 | convolution fusion | flops 5462360064 | bytes 33226752 | tf_op jit(solution)/shard_map/dot_general | solution.py:53
  302.2 16.0 %fusion.13 = f32[1024,1536]{1,0:T(8,128)} fusion(bf16[2,1536,1728]{1,2,0:T(8,128)(2,1)S(1)} %bitcast.95, bf16[1,1024,1728]{1,2,0:T(8,128)(2,1)} %get-tuple-element.150, bf16[1,1024,1728]{1,2,0:T(8,128)(2,1)} %get-tuple-element.149), kind=kOutput, calls=%fused_computation.33 | convolution fusion | flops 10875174912 | bytes 23986176 | tf_op jit(solution)/shard_map/stf,sdf->td/dot_general | solution.py:146
  318.3 10.2 convolution_convert_fusion
  328.5 211.6 %all-reduce.12.cloned.1.call-done = f32[1024,1536]{1,0:T(8,128)} async-done(((f32[1024,1536]{1,0:T(8,128)}), f32[1024,1536]{1,0:T(8,128)}) %all-reduce.12.cloned.1.call-update) | async-done | bytes 6291472 | tf_op jit(solution)/shard_map/psum | solution.py:149
  540.1 6.1 multiply_reduce_fusion
  546.8 116.2 %all-reduce.10.cloned.1.call-done = bf16[1024,1536]{1,0:T(8,128)(2,1)} async-done(((bf16[1024,1536]{1,0:T(8,128)(2,1)}), bf16[1024,1536]{1,0:T(8,128)(2,1)}) %all-reduce.10.cloned.1.call-update) | async-done | bytes 3145744 | tf_op jit(solution)/shard_map/psum | solution.py:135
  663.0 9.4 multiply_add_fusion
  678.6 19.5 %convolution_bitcast_fusion = f32[2,1536,1728]{1,2,0:T(8,128)} fusion(bf16[1,1024,1728]{1,2,0:T(8,128)(2,1)} %get-tuple-element.150, bf16[1,1024,1728]{1,2,0:T(8,128)(2,1)} %get-tuple-element.149, f32[1024,1536]{1,0:T(8,128)} %copy-done.2, f32[1536]{0:T(1024)S(1)} %get-tuple-element.115, f32[1024]{0:T(1024)S(1)} %add_rsqrt_fusion), kind=kOutput, calls=%fused_computation | convolution fusion | flops 10879893504 | bytes 34613248 | tf_op jit(solution)/shard_map/td,stf->sdf/dot_general | solution.py:143
  698.1 32.6 %copy.83 = f32[2,1536,1728]{2,0,1:T(2,128)} copy(f32[2,1536,1728]{1,2,0:T(8,128)} %convolution_bitcast_fusion) | data formatting | bytes 42467328 | tf_op jit(solution)/shard_map/td,stf->sdf/transpose | solution.py:143
  730.9 5.0 fusion.27
  747.3 6.3 convolution_bitcast_fusion.3
  753.6 11.2 fusion.55
  765.5 10.0 convolution_bitcast_fusion.2
  775.4 10.9 copy.97
  786.3 7.3 copy.104
  805.1 4.0 constant_dynamic-slice_fusion.1
  823.4 179.7 %all-reduce.16.cloned.1.call-done = f32[2,1536,1728]{2,0,1:T(2,128)} async-done(((f32[2,1536,1728]{2,0,1:T(2,128)}), f32[2,1536,1728]{2,0,1:T(2,128)}) %all-reduce.16.cloned.1.call-update) | async-done | bytes 21233680
  1003.1 6.7 multiply_reduce_fusion.3
  1009.7 218.6 %all-reduce.14.cloned.1.call-done = f32[1024,1536]{1,0:T(8,128)} async-done(((f32[1024,1536]{1,0:T(8,128)}), f32[1024,1536]{1,0:T(8,128)}) %all-reduce.14.cloned.1.call-update) | async-done | bytes 6291472 | tf_op jit(solution)/shard_map/psum | solution.py:186
  1228.3 4.7 fusion.10
  1233.6 25.3 %all-reduce.1 = (f32[3,384]{1,0:T(4,128)}, f32[2,1536]{1,0:T(2,128)}) all-reduce(f32[3,384]{1,0:T(4,128)} %pad_maximum_fusion.9, f32[2,1536]{1,0:T(2,128)} %pad_maximum_fusion.8), channel_id=1, replica_groups=mesh['dp'=8,'tensor'=4] {'dp'}, use_global_device_ids=true, to_apply=%region_19.0 | all-reduce | flops 4224 | bytes 33792 | tf_op jit(solution)/shard_map/psum | solution.py:190
  1262.9 9.6 fusion.9
  1272.5 43.3 %reduce-scatter.8.cloned.1.call-done = f32[1728,192]{0,1:T(8,128)} async-done(((f32[1728,1536]{0,1:T(8,128)}), f32[1728,192]{0,1:T(8,128)}) %reduce-scatter.8.cloned.1.call-update) | async-done | bytes 1327120 | tf_op jit(solution)/shard_map/reduce_scatter | solution.py:195
  1318.1 66.8 %reduce-scatter.10.cloned.1.call-done = f32[192,1152]{1,0:T(8,128)} async-done(((f32[1536,1152]{1,0:T(8,128)}), f32[192,1152]{1,0:T(8,128)}) %reduce-scatter.10.cloned.1.call-update) | async-done | bytes 884752
  1396.6 39.2 %psum.55 = f32[]{:T(128)} all-reduce(f32[]{:T(128)S(6)} %add.202), channel_id=1, replica_groups=mesh['dp'=8,'tensor'=4] {'dp','tensor'}, use_global_device_ids=true, to_apply=%region_25.0 | all-reduce | flops 1 | bytes 8 | tf_op jit(solution)/shard_map/psum | solution.py:205
  1436.6 4.6 add_multiply_fusion.2
  1451.6 8.9 add_multiply_fusion
  (164 shorter events, 96.5 us)
Async XLA Ops:
  7.2 254.4 %all-reduce.8.cloned.1.call-start = ((), (), s32[]{:S(2)}) async-start(), calls=%async_computation.3 | async-start | bytes 12582912 | tf_op jit(solution)/shard_map/psum | solution.py:123
  8.2 7.4 copy-start.24
  19.4 6.6 collective-permute-start
  23.0 8.2 copy-start.32
  26.0 5.2 copy-start.27
  36.6 503.5 %all-reduce.12.cloned.1.call-start = ((), (), s32[]{:S(2)}) async-start(), calls=%async_computation.5 | async-start | bytes 12582912 | tf_op jit(solution)/shard_map/psum | solution.py:149
  268.9 17.3 %copy-start.13 = (bf16[1024,1536]{1,0:T(8,128)(2,1)S(1)}, bf16[1024,1536]{1,0:T(8,128)(2,1)}, u32[]{:S(2)}) copy-start(bf16[1024,1536]{1,0:T(8,128)(2,1)} %param.23) | copy-start | bytes 9437188
  268.9 33.3 %slice-start = ((s8[10616832]{0:T(1024)(128)(4,1)}), s8[2228224]{0:T(1024)(128)(4,1)S(1)}, s32[]{:S(2)}) async-start(s8[10616832]{0:T(1024)(128)(4,1)} %bitcast.94), calls=%async_computation.11 | async-start | bytes 4456448
  268.9 33.3 %slice-start.1 = ((s8[10616832]{0:T(1024)(128)(4,1)}), s8[4194304]{0:T(1024)(128)(4,1)S(1)}, s32[]{:S(2)}) async-start(s8[10616832]{0:T(1024)(128)(4,1)} %bitcast.94), calls=%async_computation.12 | async-start | bytes 8388608
  286.2 16.0 %slice-start.2 = ((s8[10616832]{0:T(1024)(128)(4,1)}), s8[4194304]{0:T(1024)(128)(4,1)S(1)}, s32[]{:S(2)}) async-start(s8[10616832]{0:T(1024)(128)(4,1)} %bitcast.94), calls=%async_computation.13 | async-start | bytes 8388608
  318.2 344.8 %all-reduce.10.cloned.1.call-start = ((), (), s32[]{:S(2)}) async-start(), calls=%async_computation.4 | async-start | bytes 6291456 | tf_op jit(solution)/shard_map/psum | solution.py:135
  328.5 493.3 %reduce-scatter.6.cloned.1.call-start = ((), (), s32[]{:S(2)}) async-start(), calls=%async_computation.7 | async-start | bytes 2654208 | tf_op jit(solution)/shard_map/reduce_scatter | solution.py:193
  663.0 12.1 copy-start.8
  678.4 324.7 %all-reduce.16.cloned.1.call-start = ((), (), s32[]{:S(2)}) async-start(), calls=%async_computation.10 | async-start | bytes 44040192
  730.8 497.5 %all-reduce.14.cloned.1.call-start = ((), (), s32[]{:S(2)}) async-start(), calls=%async_computation.6 | async-start | bytes 12582912 | tf_op jit(solution)/shard_map/psum | solution.py:186
  735.9 5.2 copy-start.4
  735.9 5.2 copy-start.28
  737.9 8.5 copy-start.18
  737.9 3.1 collective-permute-start.1
  753.5 562.3 %reduce-scatter.8.cloned.1.call-start = ((), (), s32[]{:S(2)}) async-start(), calls=%async_computation.8 | async-start | bytes 12386304 | tf_op jit(solution)/shard_map/reduce_scatter | solution.py:195
  764.8 620.1 %reduce-scatter.10.cloned.1.call-start = ((), (), s32[]{:S(2)}) async-start(), calls=%async_computation.9 | async-start | bytes 7962624
  809.0 12.1 copy-start.40
  1441.2 7.6 copy-start.26
  1441.2 9.0 copy-start.39
  1451.6 9.0 copy-start.17
  1451.6 9.0 copy-start.21
  1451.6 9.0 copy-start.22
  1451.6 9.0 copy-start.23
  1451.6 10.1 copy-start.11
  1451.6 10.1 copy-start.14
  1451.6 10.1 copy-start.15
  1451.6 10.0 copy-start.16
  (22 other events, 74.7 us)
Sparse Core Ops, SparseCore 0:
  36.7 224.8 all-reduce.7
  318.3 221.7 all-reduce.11
  543.1 119.9 all-reduce.9
  678.5 41.3 reduce-scatter.5
  730.9 272.1 all-reduce.15
  1005.3 222.9 all-reduce.13
  1232.4 83.3 reduce-scatter.7
  1319.3 65.4 reduce-scatter.9
where the time goes:
time: 1480 us; the launch traced here: 1470 us
  waiting for transfers between devices  1060 us (72%)
  matrix products  123 us (8%)
  local copies, waits for them, and re-layouts  106 us (7%)
  other arithmetic  89.6 us (6%)
  blocking collectives  64.6 us (4%)
  between operations  21.5 us (1%)
    unnamed x10, waiting for transfers between devices  247 us
    psum x1, waiting for transfers between devices, body(): branch = lax.psum(branch_part, 'tensor')  225 us
    psum x1, waiting for transfers between devices, body(): grad_normed_one = lax.psum(normed_one_part, 'tensor')  219 us
    psum x1, waiting for transfers between devices, body(): grad_normed_two = lax.psum(normed_two_part, 'tensor')  212 us
    psum x1, waiting for transfers between devices, body(): lax.psum(feed_part.astype(jnp.bfloat16), 'tensor').astype(jnp.float32)  116 us
    unnamed x103, local copies, waits for them, and re-layouts  58.6 us
    reduce_scatter x1, waiting for transfers between devices, body(): lax.psum_scatter(down_part, 'dp', scatter_dimension=1, tiled=True)  43.3 us
    psum x1, blocking collectives, body(): square_total = lax.psum(local_square, ('dp', 'tensor'))  39.2 us
  transfers between devices with their start and end apart: 10, of which 8 were waited for; matrix products, arithmetic and copies ran while one was open for 13% of the time, Pallas kernels for 0%

commit v1 on v0

--- a/solution.py
+++ b/solution.py
@@ -120,7 +120,9 @@
         )
     gated_rows = (streams[1] * conv_out).astype(jnp.bfloat16)
     branch_part = jnp.dot(gated_rows, mixer_weight, preferred_element_type=jnp.float32)
-    branch = lax.psum(branch_part, "tensor")
+    branch = branch_part
+    for hop in (1, 2):
+        branch = branch + lax.ppermute(branch, "tensor", [(dev, dev ^ hop) for dev in range(4)])
     middle = tokens + branch
     scale_two = rms_scale(middle)
     normal_two = middle * scale_two

time: 1480 us -> 1680 us (1.14)
  waiting for transfers between devices: 1060 us -> 1250 us
    ppermute x0 -> x2, waiting for transfers between devices: none -> 406 us  [body(): lax.ppermute(branch, 'tensor', [(dev, dev ^ hop) for dev in range(4)])]
    psum x1 -> x0, waiting for transfers between devices: 225 us -> none  [body(): branch = lax.psum(branch_part, 'tensor')]
    unnamed x103 -> x101, local copies, waits for them, and re-layouts: 58.6 us -> 55.9 us
    unnamed x10 -> x9, waiting for transfers between devices: 247 us -> 249 us
  transfers between devices with their start and end apart: 10 -> 11, of which waited for: 8 -> 9; matrix products, arithmetic and copies ran while one was open for 13% -> 11% of each run, Pallas kernels for 0% -> 0%
where the time goes in v1:
time: 1680 us; the launch traced here: 1670 us
  waiting for transfers between devices  1250 us (74%)
  matrix products  126 us (8%)
  local copies, waits for them, and re-layouts  103 us (6%)
  other arithmetic  91.2 us (5%)
  blocking collectives  64.6 us (4%)
  between operations  21.6 us (1%)
    ppermute x2, waiting for transfers between devices, body(): lax.ppermute(branch, 'tensor', [(dev, dev ^ hop) for dev in range(4)])  406 us
    unnamed x9, waiting for transfers between devices  249 us
    psum x1, waiting for transfers between devices, body(): grad_normed_one = lax.psum(normed_one_part, 'tensor')  219 us
    psum x1, waiting for transfers between devices, body(): grad_normed_two = lax.psum(normed_two_part, 'tensor')  213 us
    psum x1, waiting for transfers between devices, body(): lax.psum(feed_part.astype(jnp.bfloat16), 'tensor').astype(jnp.float32)  116 us
    unnamed x101, local copies, waits for them, and re-layouts  55.9 us
    reduce_scatter x1, waiting for transfers between devices, body(): lax.psum_scatter(down_part, 'dp', scatter_dimension=1, tiled=True)  43.5 us
    psum x1, blocking collectives, body(): square_total = lax.psum(local_square, ('dp', 'tensor'))  39.5 us
  transfers between devices with their start and end apart: 11, of which 9 were waited for; matrix products, arithmetic and copies ran while one was open for 11% of the time, Pallas kernels for 0%

profile of v1, /device:TPU:0, one launch (start us, length us, event | category | flops | bytes accessed | tf_op | source)
XLA Modules:
  0.0 1666.1 jit_solution(1936757169598449842)
XLA Ops:
  11.3 4.3 convolution_bitcast_fusion.4
  35.4 135.8 %collective-permute-done.1 = f32[1024,1536]{1,0:T(8,128)} collective-permute-done((f32[1024,1536]{1,0:T(8,128)S(1)}, f32[1024,1536]{1,0:T(8,128)}, u32[]{:S(2)}, u32[]{:S(2)}) %collective-permute-start.1) | collective-permute-done | bytes 6291488 | tf_op jit(solution)/shard_map/ppermute | solution.py:125
  171.2 4.2 add.193
  178.9 270.7 %collective-permute-done.2 = f32[1024,1536]{1,0:T(8,128)} collective-permute-done((f32[1024,1536]{1,0:T(8,128)S(1)}, f32[1024,1536]{1,0:T(8,128)}, u32[]{:S(2)}, u32[]{:S(2)}) %collective-permute-start.2) | collective-permute-done | bytes 6291488 | tf_op jit(solution)/shard_map/ppermute | solution.py:125
  449.7 6.6 multiply_reduce_fusion.2
  456.4 19.9 %convolution_bitcast_fusion.1 = f32[2,1024,1728]{1,2,0:T(8,128)} fusion(bf16[2,1536,1728]{1,2,0:T(8,128)(2,1)} %param.28, f32[1024,1536]{1,0:T(8,128)S(1)} %get-tuple-element.146, f32[1536]{0:T(1024)S(1)} %get-tuple-element.115, f32[1024]{0:T(1024)S(1)} %add_rsqrt_fusion), kind=kOutput, calls=%fused_computation.16 | convolution fusion | flops 10876354560 | bytes 31074304 | tf_op jit(solution)/shard_map/td,sdf->stf/dot_general | solution.py:130
  476.3 15.9 fusion.15
  492.2 17.4 %fusion.13 = f32[1024,1536]{1,0:T(8,128)} fusion(bf16[2,1536,1728]{1,2,0:T(8,128)(2,1)} %param.28, bf16[1,1024,1728]{1,2,0:T(8,128)(2,1)} %get-tuple-element.150, bf16[1,1024,1728]{1,2,0:T(8,128)(2,1)} %get-tuple-element.149), kind=kOutput, calls=%fused_computation.33 | convolution fusion | flops 10875174912 | bytes 23986176 | tf_op jit(solution)/shard_map/stf,sdf->td/dot_general | solution.py:148
  509.6 10.6 convolution_convert_fusion
  520.3 212.9 %all-reduce.9.cloned.1.call-done = f32[1024,1536]{1,0:T(8,128)} async-done(((f32[1024,1536]{1,0:T(8,128)}), f32[1024,1536]{1,0:T(8,128)}) %all-reduce.9.cloned.1.call-update) | async-done | bytes 6291472 | tf_op jit(solution)/shard_map/psum | solution.py:151
  733.2 6.1 multiply_reduce_fusion
  739.9 116.2 %all-reduce.7.cloned.1.call-done = bf16[1024,1536]{1,0:T(8,128)(2,1)} async-done(((bf16[1024,1536]{1,0:T(8,128)(2,1)}), bf16[1024,1536]{1,0:T(8,128)(2,1)}) %all-reduce.7.cloned.1.call-update) | async-done | bytes 3145744 | tf_op jit(solution)/shard_map/psum | solution.py:137
  856.1 9.4 multiply_add_fusion
  871.5 19.7 %convolution_bitcast_fusion = f32[2,1536,1728]{1,2,0:T(8,128)} fusion(bf16[1,1024,1728]{1,2,0:T(8,128)(2,1)} %get-tuple-element.150, bf16[1,1024,1728]{1,2,0:T(8,128)(2,1)} %get-tuple-element.149, f32[1024,1536]{1,0:T(8,128)} %copy-done.2, f32[1536]{0:T(1024)S(1)} %get-tuple-element.115, f32[1024]{0:T(1024)S(1)} %add_rsqrt_fusion), kind=kOutput, calls=%fused_computation | convolution fusion | flops 10879893504 | bytes 34613248 | tf_op jit(solution)/shard_map/td,stf->sdf/dot_general | solution.py:145
  891.2 32.7 %copy.83 = f32[2,1536,1728]{2,0,1:T(2,128)} copy(f32[2,1536,1728]{1,2,0:T(8,128)} %convolution_bitcast_fusion) | data formatting | bytes 42467328 | tf_op jit(solution)/shard_map/td,stf->sdf/transpose | solution.py:145
  924.0 6.0 fusion.32
  936.8 6.3 convolution_bitcast_fusion.3
  943.1 11.5 fusion.57
  955.3 10.0 convolution_bitcast_fusion.2
  965.3 11.2 copy.97
  976.6 7.4 copy.104
  1013.8 182.3 %all-reduce.13.cloned.1.call-done = f32[2,1536,1728]{2,0,1:T(2,128)} async-done(((f32[2,1536,1728]{2,0,1:T(2,128)}), f32[2,1536,1728]{2,0,1:T(2,128)}) %all-reduce.13.cloned.1.call-update) | async-done | bytes 21233680
  1196.1 6.7 multiply_reduce_fusion.3
  1202.8 218.6 %all-reduce.11.cloned.1.call-done = f32[1024,1536]{1,0:T(8,128)} async-done(((f32[1024,1536]{1,0:T(8,128)}), f32[1024,1536]{1,0:T(8,128)}) %all-reduce.11.cloned.1.call-update) | async-done | bytes 6291472 | tf_op jit(solution)/shard_map/psum | solution.py:188
  1421.4 4.7 fusion.10
  1426.7 25.1 %all-reduce.1 = (f32[3,384]{1,0:T(4,128)}, f32[2,1536]{1,0:T(2,128)}) all-reduce(f32[3,384]{1,0:T(4,128)} %pad_maximum_fusion.9, f32[2,1536]{1,0:T(2,128)} %pad_maximum_fusion.8), channel_id=1, replica_groups=mesh['dp'=8,'tensor'=4] {'dp'}, use_global_device_ids=true, to_apply=%region_18.0 | all-reduce | flops 4224 | bytes 33792 | tf_op jit(solution)/shard_map/psum | solution.py:192
  1455.7 9.6 fusion.9
  1465.3 43.5 %reduce-scatter.8.cloned.1.call-done = f32[1728,192]{0,1:T(8,128)} async-done(((f32[1728,1536]{0,1:T(8,128)}), f32[1728,192]{0,1:T(8,128)}) %reduce-scatter.8.cloned.1.call-update) | async-done | bytes 1327120 | tf_op jit(solution)/shard_map/reduce_scatter | solution.py:197
  1511.0 66.8 %reduce-scatter.10.cloned.1.call-done = f32[192,1152]{1,0:T(8,128)} async-done(((f32[1536,1152]{1,0:T(8,128)}), f32[192,1152]{1,0:T(8,128)}) %reduce-scatter.10.cloned.1.call-update) | async-done | bytes 884752
  1589.5 39.5 %psum.47 = f32[]{:T(128)} all-reduce(f32[]{:T(128)S(6)} %add.208), channel_id=1, replica_groups=mesh['dp'=8,'tensor'=4] {'dp','tensor'}, use_global_device_ids=true, to_apply=%region_24.0 | all-reduce | flops 1 | bytes 8 | tf_op jit(solution)/shard_map/psum | solution.py:207
  1629.8 4.6 add_multiply_fusion.2
  1644.8 8.9 add_multiply_fusion
  (163 shorter events, 99.8 us)
Async XLA Ops:
  7.2 726.0 %all-reduce.9.cloned.1.call-start = ((), (), s32[]{:S(2)}) async-start(), calls=%async_computation.4 | async-start | bytes 12582912 | tf_op jit(solution)/shard_map/psum | solution.py:151
  19.4 6.6 collective-permute-start
  33.0 138.2 %collective-permute-start.1 = (f32[1024,1536]{1,0:T(8,128)S(1)}, f32[1024,1536]{1,0:T(8,128)}, u32[]{:S(2)}, u32[]{:S(2)}) collective-permute-start(f32[1024,1536]{1,0:T(8,128)S(1)} %fusion.56), channel_id=1, source_target_pairs={{0,1},{1,0},{2,3},{3,2},{4,5},{5,4},{6,7},{7,6},{8,9},{9,8},{10,11... | collective-permute-start | bytes 18874376 | tf_op jit(solution)/shard_map/ppermute | solution.py:125
  175.4 274.3 %collective-permute-start.2 = (f32[1024,1536]{1,0:T(8,128)S(1)}, f32[1024,1536]{1,0:T(8,128)}, u32[]{:S(2)}, u32[]{:S(2)}) collective-permute-start(f32[1024,1536]{1,0:T(8,128)S(1)} %add.193), channel_id=1, source_target_pairs={{0,2},{1,3},{2,0},{3,1},{4,6},{5,7},{6,4},{7,5},{8,10},{9,11},{10,... | collective-permute-start | bytes 18874376 | tf_op jit(solution)/shard_map/ppermute | solution.py:125
  456.3 20.0 %copy-start.2 = (f32[1024,1536]{1,0:T(8,128)}, f32[1024,1536]{1,0:T(8,128)S(1)}, u32[]{:S(2)}) copy-start(f32[1024,1536]{1,0:T(8,128)S(1)} %get-tuple-element.146) | copy-start | bytes 18874372
  456.3 20.0 %copy-start.13 = (bf16[1024,1536]{1,0:T(8,128)(2,1)S(1)}, bf16[1024,1536]{1,0:T(8,128)(2,1)}, u32[]{:S(2)}) copy-start(bf16[1024,1536]{1,0:T(8,128)(2,1)} %param.23) | copy-start | bytes 9437188
  509.6 346.5 %all-reduce.7.cloned.1.call-start = ((), (), s32[]{:S(2)}) async-start(), calls=%async_computation.3 | async-start | bytes 6291456 | tf_op jit(solution)/shard_map/psum | solution.py:137
  520.2 492.0 %reduce-scatter.6.cloned.1.call-start = ((), (), s32[]{:S(2)}) async-start(), calls=%async_computation.6 | async-start | bytes 2654208 | tf_op jit(solution)/shard_map/reduce_scatter | solution.py:195
  856.1 12.1 copy-start.9
  871.5 324.7 %all-reduce.13.cloned.1.call-start = ((), (), s32[]{:S(2)}) async-start(), calls=%async_computation.9 | async-start | bytes 44040192
  923.9 497.5 %all-reduce.11.cloned.1.call-start = ((), (), s32[]{:S(2)}) async-start(), calls=%async_computation.5 | async-start | bytes 12582912 | tf_op jit(solution)/shard_map/psum | solution.py:188
  923.9 9.4 slice-start
  923.9 9.4 slice-start.1
  923.9 9.4 copy-start.28
  923.9 9.4 copy-start.33
  924.0 9.4 copy-start.34
  924.0 9.4 copy-start.35
  924.0 9.4 copy-start.36
  924.0 9.4 copy-start.37
  930.0 3.2 collective-permute-start.3
  943.1 565.6 %reduce-scatter.8.cloned.1.call-start = ((), (), s32[]{:S(2)}) async-start(), calls=%async_computation.7 | async-start | bytes 12386304 | tf_op jit(solution)/shard_map/reduce_scatter | solution.py:197
  954.6 623.2 %reduce-scatter.10.cloned.1.call-start = ((), (), s32[]{:S(2)}) async-start(), calls=%async_computation.8 | async-start | bytes 7962624
  999.4 12.1 copy-start.40
  1634.4 9.0 copy-start.39
  1644.8 9.0 copy-start.17
  1644.8 9.0 copy-start.21
  1644.8 9.0 copy-start.22
  1644.8 9.0 copy-start.23
  1644.8 10.1 copy-start.11
  1644.8 10.1 copy-start.14
  1644.8 10.1 copy-start.15
  1644.8 10.0 copy-start.16
  (22 other events, 81.5 us)
Sparse Core Ops, SparseCore 0:
  509.7 223.4 all-reduce.8
  736.1 119.9 all-reduce.6
  871.6 41.3 reduce-scatter.5
  924.0 272.1 all-reduce.12
  1198.4 222.9 all-reduce.10
  1425.4 83.3 reduce-scatter.7
  1512.2 65.4 reduce-scatter.9
